TPU v7x, 256 devices: a whole 4x4x8 slice. The times are simulated.
256 devices in a mesh: rows: 64 (over x, z, y_hi), cols: 4 (over y_lo, core).
Axes of the slice: x: 4, y: 4 (y_hi: 2, y_lo: 2; y = y_hi * 2 + y_lo), z: 8, core: 2. Of those that a mesh axis runs over, the one named last changes fastest.
Arguments:
- matrix: float32 [4096, 32, 2, 128], P('rows', 'cols'), may hold values from -54 to 54
- plan: int32 [2, 4, 256], replicated, may hold values from 0 to 255, as said below
Outputs:
- rotated: float32 [4096, 32, 2, 128], P('rows', 'cols')
Inputs may be any that keep to these rules, and one draw needn't show every extreme that they name: Each plan[s, r] pairs the 256 columns: partner of partner of i is i, and no column is its own partner.
All inputs are finite; a program needn't handle non-finite values.
Results may differ from a plain program's by a relative error of at most 0.0003.
Values sent between devices are 32-bit elements; how exact they have to be, the bound alone decides.
A program may use at most 128 MiB of HBM per device.

v0:
```python
import jax
import jax.numpy as jnp
from jax import lax
from jax.sharding import Mesh
from jax.sharding import PartitionSpec as P

STEPS = 2
ROWS = ("rows_0", "rows_1", "rows_2")


def padded_to(lines, devices):
    spare = -len(lines) % devices
    return jnp.pad(lines, [(0, spare)] + [(0, 0)] * (lines.ndim - 1))


def sent_to_all(value, axis):
    copies = jnp.broadcast_to(value, (lax.axis_size(axis), *value.shape))
    return lax.all_to_all(copies, axis, split_axis=0, concat_axis=0, tiled=True)


def joined_along(blocks, dim):
    lengths = list(blocks.shape[1:])
    lengths[dim] *= blocks.shape[0]
    return jnp.moveaxis(blocks, 0, dim).reshape(lengths)


def whole_of(value, axes, dim):
    far, near = axes
    blocks = sent_to_all(sent_to_all(value, far), near)
    return joined_along(blocks.swapaxes(0, 1).reshape(-1, *value.shape), dim)


def split_up(value, dim, devices):
    lengths = value.shape
    blocks = value.reshape(*lengths[:dim], devices, lengths[dim] // devices, *lengths[dim + 1 :])
    return jnp.moveaxis(blocks, dim, 0)


def summed_on_arrival(value, axis, dim):
    blocks = split_up(value, dim, lax.axis_size(axis))
    arrived = lax.all_to_all(blocks, axis, split_axis=0, concat_axis=0, tiled=True)
    return arrived.sum(axis=0)


def summed_rows(value, axes, dim):
    far, near = axes
    own = summed_on_arrival(split_up(value, dim, lax.axis_size(far)), near, dim + 1)
    return jnp.sum(lax.all_to_all(own, far, 0, 0, tiled=True), axis=0)


def total_of(value, axes):
    lines = value.reshape(-1, value.shape[-1])
    padded = padded_to(lines, lax.axis_size(axes[0]) * lax.axis_size(axes[1]))
    whole = whole_of(summed_rows(padded, axes, 0), axes, 0)
    return lax.slice_in_dim(whole, 0, len(lines)).reshape(value.shape)


def passed_along(block, axis, distance):
    devices = range(lax.axis_size(axis))
    route = [((i - distance) % len(devices), i) for i in devices]
    return lax.ppermute(block, axis, route)


def diagonalize(grams, table):
    width = grams.shape[1]
    indices = jnp.arange(width, dtype=jnp.int32)
    rotation = jnp.broadcast_to(jnp.eye(width, dtype=jnp.float32), grams.shape)
    unit_matrix = jnp.eye(width, dtype=jnp.float32)
    for round_index in range(table.shape[0]):
        partner = table[round_index]
        onehot = (partner[:, None] == indices[None, :]).astype(jnp.float32)
        diagonal_now = jnp.diagonal(grams, axis1=1, axis2=2)
        partner_diag = jnp.einsum(
            "pj,ij->pi", diagonal_now, onehot, precision=lax.Precision.HIGHEST
        )
        partner_gram = jnp.sum(grams * onehot[None], axis=2)
        orient = jnp.where(indices < partner, 1.0, -1.0).astype(jnp.float32)
        spread = orient[None, :] * (partner_diag - diagonal_now)
        sign_part = jnp.where(spread >= 0.0, 1.0, -1.0).astype(jnp.float32)
        tangent = (
            sign_part
            * 2.0
            * partner_gram
            / (jnp.abs(spread) + jnp.sqrt(spread * spread + 4.0 * partner_gram * partner_gram))
        )
        cosine = 1.0 / jnp.sqrt(1.0 + tangent * tangent)
        sine_part = tangent * cosine
        off_part = jnp.swapaxes(onehot[None] * (-orient[None, :] * sine_part)[:, :, None], 1, 2)
        rot_now = cosine[:, :, None] * unit_matrix[None] + off_part
        product = jnp.einsum("pij,pjk->pik", grams, rot_now, precision=lax.Precision.HIGHEST)
        grams = jnp.einsum("pji,pjk->pik", rot_now, product, precision=lax.Precision.HIGHEST)
        rotation = jnp.einsum("pij,pjk->pik", rotation, rot_now, precision=lax.Precision.HIGHEST)
    return (grams, rotation)


def full_grams(columns):
    local_sum = jnp.einsum("mpi,mpj->pij", columns, columns, precision=lax.Precision.HIGHEST)
    return total_of(local_sum, (("rows_0", "rows_1"), "rows_2"))


def body(matrix, plan):
    rows_here, pair_here, halves, width = matrix.shape
    columns = matrix.reshape(rows_here, pair_here, halves * width)
    grams = full_grams(columns)
    for step_index in range(STEPS):
        grams, rotation = diagonalize(grams, plan[step_index])
        columns = jnp.einsum("mpi,pij->mpj", columns, rotation, precision=lax.Precision.HIGHEST)
        quarter = columns.reshape(rows_here, pair_here, halves, width)
        tops = quarter[:, :, 0, :]
        bottoms = quarter[:, :, 1, :]
        bottoms = passed_along(bottoms, "cols", 1)
        columns = jnp.stack([tops, bottoms], axis=2).reshape(rows_here, pair_here, halves * width)
        if step_index + 1 < STEPS:
            grams = full_grams(columns)
    return columns.reshape(matrix.shape)


def solution(mesh):
    split = Mesh(
        mesh.devices.reshape(4, 8, 2, mesh.shape["cols"]), ("rows_0", "rows_1", "rows_2", "cols")
    )
    in_specs = (P(ROWS, "cols", None, None), P())
    out_specs = P(ROWS, "cols", None, None)
    return jax.shard_map(body, mesh=split, in_specs=in_specs, out_specs=out_specs, check_vma=False)
```

profile of v0, /device:TPU:1, one launch (start us, length us, event | category | flops | bytes accessed | tf_op | source)
XLA Modules:
  0.0 514.9 jit_solution(14729319137601983196)
XLA Ops:
  3.6 30.3 %all_to_all.40 = f32[2,32,32,256]{3,2,1,0:T(8,128)S(1)} all-to-all(f32[2,32,32,256]{3,2,1,0:T(8,128)S(1)} %bitcast.132), channel_id=1, replica_groups=mesh['rows_0'=4,'rows_1'=8,'rows_2'=2,'cols'=4] {'rows_2'}, dimensions={0} | all-to-all | bytes 4194304 | tf_op jit(solution)/shard_map/all_to_all | solution.py:41
  35.1 35.5 %all_to_all.41 = f32[32,32,256]{2,1,0:T(8,128)S(1)} all-to-all(f32[32,32,256]{2,1,0:T(8,128)} %reduce_sum.112), channel_id=1, replica_groups=mesh['rows_0'=4,'rows_1'=8,'rows_2'=2,'cols'=4] {'rows_0','rows_1'}, dimensions={0} | all-to-all | bytes 2097152 | tf_op jit(solution)/shard_map/all_to_all | solution.py:48
  71.8 8.1 %all-to-all-start.2 = ((f32[32,32,256]{2,1,0:T(8,128)}), f32[32,32,256]{2,1,0:T(8,128)S(1)}, u32[]{:S(2)}, u32[]{:S(2)}) async-start(f32[32,32,256]{2,1,0:T(8,128)} %broadcast_in_dim.161), calls=%async_computation.2 | async-start | bytes 2097152 | tf_op jit(solution)/shard_map/all_to_all | solution.py:18
  83.8 20.7 %all-to-all-done.2 = f32[32,32,256]{2,1,0:T(8,128)S(1)} async-done(((f32[32,32,256]{2,1,0:T(8,128)}), f32[32,32,256]{2,1,0:T(8,128)S(1)}, u32[]{:S(2)}, u32[]{:S(2)}) %all-to-all-start.2) | async-done | bytes 1048608 | tf_op jit(solution)/shard_map/all_to_all | solution.py:18
  113.0 18.3 %all-to-all-done.3 = f32[2,32,32,256]{3,2,1,0:T(8,128)S(1)} async-done(((f32[2,32,32,256]{3,2,1,0:T(8,128)}), f32[2,32,32,256]{3,2,1,0:T(8,128)S(1)}, u32[]{:S(2)}, u32[]{:S(2)}) %all-to-all-start.3) | async-done | bytes 2097184 | tf_op jit(solution)/shard_map/all_to_all | solution.py:18
  135.0 16.3 %copy.88 = f32[8,256,256]{0,2,1:T(8,128)} copy(f32[8,256,256]{2,1,0:T(8,128)S(1)} %bitcast.127) | data formatting | bytes 4194304 | tf_op jit(solution)/shard_map/reshape;reshape;reshape | solution.py:55
  155.3 5.0 fusion.26
  167.2 16.5 %copy.91 = f32[8,256,256]{0,2,1:T(8,128)} copy(f32[8,256,256]{1,2,0:T(8,128)S(1)} %get-tuple-element.54) | data formatting | bytes 4194304 | tf_op jit(solution)/shard_map/pji,pjk->pik/dot_general | solution.py:91
  195.1 16.7 %copy.95 = f32[8,256,256]{0,2,1:T(8,128)} copy(f32[8,256,256]{1,2,0:T(8,128)S(1)} %get-tuple-element.56) | data formatting | bytes 4194304 | tf_op jit(solution)/shard_map/pji,pjk->pik/dot_general | solution.py:91
  222.7 16.5 %copy.99 = f32[8,256,256]{0,2,1:T(8,128)} copy(f32[8,256,256]{1,2,0:T(8,128)S(1)} %get-tuple-element.58) | data formatting | bytes 4194304 | tf_op jit(solution)/shard_map/pji,pjk->pik/dot_general | solution.py:91
  241.6 4.1 fusion.24
  253.5 6.4 %collective-permute-start = (f32[64,8,128]{2,0,1:T(8,128)S(1)}, f32[64,8,128]{2,0,1:T(8,128)S(1)}, u32[]{:S(2)}, u32[]{:S(2)}) collective-permute-start(f32[64,8,128]{2,0,1:T(8,128)S(1)} %bitcast.140), channel_id=1, source_target_pairs={{3,0},{0,1},{1,2},{2,3},{7,4},{4,5},{5,6},{6,7},{11,8},{8,9},{9,10... | collective-permute-start | bytes 786440 | tf_op jit(solution)/shard_map/ppermute | solution.py:61
  265.4 26.8 %all_to_all.42 = f32[2,32,32,256]{3,2,1,0:T(8,128)S(1)} all-to-all(f32[2,32,32,256]{3,2,1,0:T(8,128)S(1)} %bitcast.134), channel_id=1, replica_groups=mesh['rows_0'=4,'rows_1'=8,'rows_2'=2,'cols'=4] {'rows_2'}, dimensions={0} | all-to-all | bytes 4194304 | tf_op jit(solution)/shard_map/all_to_all | solution.py:41
  292.4 29.4 %all_to_all.43 = f32[32,32,256]{2,1,0:T(8,128)S(1)} all-to-all(f32[32,32,256]{2,1,0:T(8,128)S(1)} %reduce_sum.119), channel_id=1, replica_groups=mesh['rows_0'=4,'rows_1'=8,'rows_2'=2,'cols'=4] {'rows_0','rows_1'}, dimensions={0} | all-to-all | bytes 2097152 | tf_op jit(solution)/shard_map/all_to_all | solution.py:48
  323.0 9.2 %all-to-all-start.6 = ((f32[32,32,256]{2,1,0:T(8,128)}), f32[32,32,256]{2,1,0:T(8,128)S(1)}, u32[]{:S(2)}, u32[]{:S(2)}) async-start(f32[32,32,256]{2,1,0:T(8,128)} %broadcast_in_dim.164), calls=%async_computation.6 | async-start | bytes 2097152 | tf_op jit(solution)/shard_map/all_to_all | solution.py:18
  335.4 18.1 %all-to-all-done.6 = f32[32,32,256]{2,1,0:T(8,128)S(1)} async-done(((f32[32,32,256]{2,1,0:T(8,128)}), f32[32,32,256]{2,1,0:T(8,128)S(1)}, u32[]{:S(2)}, u32[]{:S(2)}) %all-to-all-start.6) | async-done | bytes 1048608 | tf_op jit(solution)/shard_map/all_to_all | solution.py:18
  355.2 5.0 all-to-all-start.7
  362.4 16.0 %all-to-all-done.7 = f32[2,32,32,256]{3,2,1,0:T(8,128)} async-done(((f32[2,32,32,256]{3,2,1,0:T(8,128)}), f32[2,32,32,256]{3,2,1,0:T(8,128)}, u32[]{:S(2)}, u32[]{:S(2)}) %all-to-all-start.7) | async-done | bytes 2097184 | tf_op jit(solution)/shard_map/all_to_all | solution.py:18
  380.2 16.3 %copy.106 = f32[8,256,256]{0,2,1:T(8,128)} copy(f32[8,256,256]{2,1,0:T(8,128)S(1)} %bitcast.125) | data formatting | bytes 4194304 | tf_op jit(solution)/shard_map/reshape;reshape;reshape | solution.py:55
  415.4 16.7 %copy.109 = f32[8,256,256]{0,2,1:T(8,128)} copy(f32[8,256,256]{1,2,0:T(8,128)S(1)} %get-tuple-element.60) | data formatting | bytes 4194304 | tf_op jit(solution)/shard_map/pji,pjk->pik/dot_general | solution.py:91
  441.7 16.5 %copy.113 = f32[8,256,256]{0,2,1:T(8,128)} copy(f32[8,256,256]{1,2,0:T(8,128)S(1)} %get-tuple-element.62) | data formatting | bytes 4194304 | tf_op jit(solution)/shard_map/pji,pjk->pik/dot_general | solution.py:91
  467.7 16.5 %copy.117 = f32[8,256,256]{0,2,1:T(8,128)} copy(f32[8,256,256]{1,2,0:T(8,128)S(1)} %get-tuple-element.64) | data formatting | bytes 4194304 | tf_op jit(solution)/shard_map/pji,pjk->pik/dot_general | solution.py:91
  486.7 4.1 fusion.11
  498.5 11.6 %collective-permute-start.1 = (f32[64,8,128]{2,1,0:T(8,128)S(1)}, f32[64,8,128]{2,1,0:T(8,128)S(1)}, u32[]{:S(2)}, u32[]{:S(2)}) collective-permute-start(f32[64,8,128]{2,1,0:T(8,128)S(1)} %bitcast.139), channel_id=1, source_target_pairs={{3,0},{0,1},{1,2},{2,3},{7,4},{4,5},{5,6},{6,7},{11,8},{8,9},{9,10... | collective-permute-start | bytes 786440 | tf_op jit(solution)/shard_map/ppermute | solution.py:61
  (173 shorter events, 133.2 us)
Async XLA Ops:
  70.6 9.3 %copy-start.29 = (s32[2,4,256]{2,1,0:T(4,128)S(1)}, s32[2,4,256]{2,1,0:T(4,128)}, u32[]{:S(2)}) copy-start(s32[2,4,256]{2,1,0:T(4,128)} %param.3) | copy-start | bytes 24580
  71.8 32.7 %all-to-all-start.2 = ((f32[32,32,256]{2,1,0:T(8,128)}), f32[32,32,256]{2,1,0:T(8,128)S(1)}, u32[]{:S(2)}, u32[]{:S(2)}) async-start(f32[32,32,256]{2,1,0:T(8,128)} %broadcast_in_dim.161), calls=%async_computation.2 | async-start | bytes 2097152 | tf_op jit(solution)/shard_map/all_to_all | solution.py:18
  80.6 25.6 %copy-start.27 = (s32[1,1,256]{2,1,0:T(1,128)}, s32[1,1,256]{2,1,0:T(1,128)S(1)}, u32[]{:S(2)}) copy-start(s32[1,1,256]{2,1,0:T(1,128)S(1)} %get-tuple-element.15) | copy-start | bytes 3076
  80.6 30.1 %copy-start.26 = (s32[1,1,256]{2,1,0:T(1,128)}, s32[1,1,256]{2,1,0:T(1,128)S(1)}, u32[]{:S(2)}) copy-start(s32[1,1,256]{2,1,0:T(1,128)S(1)} %get-tuple-element.14) | copy-start | bytes 3076
  80.6 30.9 %copy-start.24 = (s32[1,1,256]{2,1,0:T(1,128)}, s32[1,1,256]{2,1,0:T(1,128)S(1)}, u32[]{:S(2)}) copy-start(s32[1,1,256]{2,1,0:T(1,128)S(1)} %get-tuple-element.13) | copy-start | bytes 3076
  80.6 31.6 %copy-start.28 = (s32[1,1,256]{2,1,0:T(1,128)}, s32[1,1,256]{2,1,0:T(1,128)S(1)}, u32[]{:S(2)}) copy-start(s32[1,1,256]{2,1,0:T(1,128)S(1)} %get-tuple-element.16) | copy-start | bytes 3076
  106.1 25.2 %all-to-all-start.3 = ((f32[2,32,32,256]{3,2,1,0:T(8,128)}), f32[2,32,32,256]{3,2,1,0:T(8,128)S(1)}, u32[]{:S(2)}, u32[]{:S(2)}) async-start(f32[2,32,32,256]{3,2,1,0:T(8,128)} %broadcast_in_dim.162), calls=%async_computation.3 | async-start | bytes 4194304 | tf_op jit(solution)/shard_map/all_to_all | solution.py:18
  155.3 5.0 copy-start.1
  222.7 18.9 %copy-start.14 = (f32[8,256]{1,0:T(8,128)S(1)}, f32[8,256]{1,0:T(8,128)}, u32[]{:S(2)}) copy-start(f32[8,256]{1,0:T(8,128)} %copy-done.13) | copy-start | bytes 24580
  241.6 4.1 copy-start.18
  253.5 11.6 %copy-start.2 = (f32[64,8,1,128]{3,2,0,1:T(1,128)}, f32[64,8,1,128]{3,2,0,1:T(1,128)S(1)}, u32[]{:S(2)}) copy-start(f32[64,8,1,128]{3,2,0,1:T(1,128)S(1)} %get-tuple-element.7) | copy-start | bytes 786436
  253.5 9.7 %collective-permute-start = (f32[64,8,128]{2,0,1:T(8,128)S(1)}, f32[64,8,128]{2,0,1:T(8,128)S(1)}, u32[]{:S(2)}, u32[]{:S(2)}) collective-permute-start(f32[64,8,128]{2,0,1:T(8,128)S(1)} %bitcast.140), channel_id=1, source_target_pairs={{3,0},{0,1},{1,2},{2,3},{7,4},{4,5},{5,6},{6,7},{11,8},{8,9},{9,10... | collective-permute-start | bytes 786440 | tf_op jit(solution)/shard_map/ppermute | solution.py:61
  321.8 10.4 %copy-start.23 = (s32[1,1,256]{2,1,0:T(1,128)S(1)}, s32[1,1,256]{2,1,0:T(1,128)}, u32[]{:S(2)}) copy-start(s32[1,1,256]{2,1,0:T(1,128)} %get-tuple-element.17) | copy-start | bytes 3076
  321.8 10.9 %copy-start.21 = (s32[1,1,256]{2,1,0:T(1,128)S(1)}, s32[1,1,256]{2,1,0:T(1,128)}, u32[]{:S(2)}) copy-start(s32[1,1,256]{2,1,0:T(1,128)} %get-tuple-element.12) | copy-start | bytes 3076
  321.8 11.5 %copy-start.19 = (s32[1,1,256]{2,1,0:T(1,128)S(1)}, s32[1,1,256]{2,1,0:T(1,128)}, u32[]{:S(2)}) copy-start(s32[1,1,256]{2,1,0:T(1,128)} %get-tuple-element.18) | copy-start | bytes 3076
  323.0 30.5 %all-to-all-start.6 = ((f32[32,32,256]{2,1,0:T(8,128)}), f32[32,32,256]{2,1,0:T(8,128)S(1)}, u32[]{:S(2)}, u32[]{:S(2)}) async-start(f32[32,32,256]{2,1,0:T(8,128)} %broadcast_in_dim.164), calls=%async_computation.6 | async-start | bytes 2097152 | tf_op jit(solution)/shard_map/all_to_all | solution.py:18
  355.2 23.2 %all-to-all-start.7 = ((f32[2,32,32,256]{3,2,1,0:T(8,128)}), f32[2,32,32,256]{3,2,1,0:T(8,128)}, u32[]{:S(2)}, u32[]{:S(2)}) async-start(f32[2,32,32,256]{3,2,1,0:T(8,128)} %broadcast_in_dim.165), calls=%async_computation.7 | async-start | bytes 4194304 | tf_op jit(solution)/shard_map/all_to_all | solution.py:18
  415.4 19.1 %copy-start.22 = (s32[1,1,256]{2,1,0:T(1,128)S(1)}, s32[1,1,256]{2,1,0:T(1,128)}, u32[]{:S(2)}) copy-start(s32[1,1,256]{2,1,0:T(1,128)} %get-tuple-element.12) | copy-start | bytes 3076
  415.4 19.1 %copy-start.36 = (f32[256]{0:T(256)S(1)}, f32[256]{0:T(256)}, u32[]{:S(2)}) copy-start(f32[256]{0:T(256)} %get-tuple-element.37) | copy-start | bytes 3076
  415.4 19.1 %copy-start.37 = (f32[256]{0:T(256)S(1)}, f32[256]{0:T(256)}, u32[]{:S(2)}) copy-start(f32[256]{0:T(256)} %get-tuple-element.38) | copy-start | bytes 3076
  441.7 18.9 %copy-start.20 = (s32[1,1,256]{2,1,0:T(1,128)S(1)}, s32[1,1,256]{2,1,0:T(1,128)}, u32[]{:S(2)}) copy-start(s32[1,1,256]{2,1,0:T(1,128)} %get-tuple-element.18) | copy-start | bytes 3076
  441.7 18.9 %copy-start.34 = (f32[256]{0:T(256)S(1)}, f32[256]{0:T(256)}, u32[]{:S(2)}) copy-start(f32[256]{0:T(256)} %get-tuple-element.35) | copy-start | bytes 3076
  441.7 18.9 %copy-start.35 = (f32[256]{0:T(256)S(1)}, f32[256]{0:T(256)}, u32[]{:S(2)}) copy-start(f32[256]{0:T(256)} %get-tuple-element.36) | copy-start | bytes 3076
  498.5 14.9 %collective-permute-start.1 = (f32[64,8,128]{2,1,0:T(8,128)S(1)}, f32[64,8,128]{2,1,0:T(8,128)S(1)}, u32[]{:S(2)}, u32[]{:S(2)}) collective-permute-start(f32[64,8,128]{2,1,0:T(8,128)S(1)} %bitcast.139), channel_id=1, source_target_pairs={{3,0},{0,1},{1,2},{2,3},{7,4},{4,5},{5,6},{6,7},{11,8},{8,9},{9,10... | collective-permute-start | bytes 786440 | tf_op jit(solution)/shard_map/ppermute | solution.py:61
  (20 other events, 64.1 us)
where the time goes:
time: 522 us; the launch traced here: 515 us
  local copies, waits for them, and re-layouts  170 us (33%)
  blocking collectives  122 us (23%)
  matrix products  80.2 us (15%)
  waiting for transfers between devices  79.8 us (15%)
  starting transfers between devices  44.2 us (8%)
  other arithmetic  17.6 us (3%)
    dot_general x6, local copies, waits for them, and re-layouts, diagonalize(): jnp.einsum('pji,pjk->pik', rot_now, product, precision=lax.Precision.HIGH...  99.4 us
    all_to_all x4, waiting for transfers between devices, sent_to_all(): return lax.all_to_all(copies, axis, split_axis=0, concat_axis=0, tiled=True)  73.1 us
    all_to_all x2, blocking collectives, summed_rows(): return jnp.sum(lax.all_to_all(own, far, 0, 0, tiled=True), axis=0)  64.9 us
    all_to_all x2, blocking collectives, summed_on_arrival(): lax.all_to_all(blocks, axis, split_axis=0, concat_axis=0, tiled=True)  57 us
    another operation x2, local copies, waits for them, and re-layouts, total_of(): return lax.slice_in_dim(whole, 0, len(lines)).reshape(value.shape)  32.6 us
    all_to_all x4, starting transfers between devices, sent_to_all(): return lax.all_to_all(copies, axis, split_axis=0, concat_axis=0, tiled=True)  26.3 us
    dot_general x6, matrix products, diagonalize(): jnp.einsum('pij,pjk->pik', grams, rot_now, precision=lax.Precision.HIGHEST)  25.3 us
    dot_general x8, matrix products, diagonalize(): jnp.einsum('pij,pjk->pik', rotation, rot_now, precision=lax.Precision.HIG...  25.1 us
  transfers between devices with their start and end apart: 6, of which 6 were waited for; matrix products, arithmetic and copies ran while one was open for 2% of the time, Pallas kernels for 0%

commit v1 on v0

v1 whole, which is shorter than its diff:
```python
import functools

import jax
import jax.numpy as jnp
from jax import lax
from jax.experimental import pallas as pl
from jax.experimental.pallas import tpu as pltpu
from jax.sharding import PartitionSpec as P

MESH = pl.DeviceIdType.MESH
XS, ZS, YS, CS = 4, 8, 2, 4
GROUP = XS * YS
BLOCK = 128
WIDTH = 2 * BLOCK
PEERS = ((2, 1), (1, 1), (3, 1), (2, 0), (0, 1), (1, 0), (3, 0))
RING = (4, 3, 5, 2, 6, 1, 7)
FIRST = (((0,), (0,)), ((), ()))
PLAIN = (((1,), (0,)), ((), ()))


def parts_of(value):
    high = value.astype(jnp.bfloat16)
    rest = value - high.astype(jnp.float32)
    middle = rest.astype(jnp.bfloat16)
    low = (rest - middle.astype(jnp.float32)).astype(jnp.bfloat16)
    return high, middle, low


def product(a, b, dims):
    return lax.dot_general(a, b, dims, preferred_element_type=jnp.float32)


def full_product(a, b, dims=PLAIN):
    return lax.dot_general(
        a, b, dims, precision=lax.Precision.HIGHEST, preferred_element_type=jnp.float32
    )


def times_onehot(parts, onehot):
    high, middle, low = parts
    return product(high, onehot, PLAIN) + (product(middle, onehot, PLAIN) + product(low, onehot, PLAIN))


def onehot_times(onehot, parts):
    high, middle, low = parts
    return product(onehot, high, PLAIN) + (product(onehot, middle, PLAIN) + product(onehot, low, PLAIN))


def solve(gram, plan_of_round, rounds, final_gram):
    below = lax.broadcasted_iota(jnp.int32, (WIDTH, WIDTH), 0)
    along = lax.broadcasted_iota(jnp.int32, (WIDTH, WIDTH), 1)
    unit = below == along
    index = lax.broadcasted_iota(jnp.int32, (1, WIDTH), 1)
    rotation = None
    for r in range(rounds):
        partner = plan_of_round(r)
        pairing = below == partner
        onehot = pairing.astype(jnp.float32).astype(jnp.bfloat16)
        moved = times_onehot(parts_of(gram), onehot)
        own = jnp.sum(jnp.where(unit, gram, 0.0), axis=0, keepdims=True)
        cross = jnp.sum(jnp.where(pairing, gram, 0.0), axis=0, keepdims=True)
        other = jnp.sum(jnp.where(pairing, moved, 0.0), axis=0, keepdims=True)
        orient = jnp.where(index < partner, 1.0, -1.0)
        spread = orient * (other - own)
        sign = jnp.where(spread >= 0.0, 1.0, -1.0)
        tangent = sign * 2.0 * cross / (jnp.abs(spread) + jnp.sqrt(spread * spread + 4.0 * cross * cross))
        cosine = 1.0 / jnp.sqrt(1.0 + tangent * tangent)
        sine = -orient * (tangent * cosine)
        if r + 1 < rounds or final_gram:
            both = onehot_times(onehot, parts_of(moved))
            cosine_down = jnp.transpose(jnp.broadcast_to(cosine, (BLOCK, WIDTH)))
            sine_down = jnp.transpose(jnp.broadcast_to(sine, (BLOCK, WIDTH)))
            cosine_down = jnp.concatenate([cosine_down, cosine_down], axis=1)
            sine_down = jnp.concatenate([sine_down, sine_down], axis=1)
            gram = (cosine_down * cosine * gram + sine_down * sine * both) + (
                cosine_down * sine * moved + sine_down * cosine * jnp.transpose(moved)
            )
        if rotation is None:
            rotation = jnp.where(unit, cosine, 0.0) + jnp.where(pairing, sine, 0.0)
        else:
            rotation = rotation * cosine + times_onehot(parts_of(rotation), onehot) * sine
    return gram, rotation


def kernel(
    x_hbm,
    plan_hbm,
    out_hbm,
    plan_ref,
    x_own,
    tops,
    bottoms,
    partial,
    shares_tt,
    shares_b,
    total,
    total_mine,
    bottoms_out,
    bottoms_in,
    square_out,
    square_in,
    tops_now,
    partial_tb,
    shares_tb,
    total_tb,
    total_tb_mine,
    result_out,
    result_in,
    load_sem,
    in_send,
    in_recv,
    sum_send,
    sum_recv,
    all_send,
    all_recv,
    next_send,
    next_recv,
    sum2_send,
    sum2_recv,
    all2_send,
    all2_recv,
    out_send,
    out_recv,
    store_sem,
):
    rows = lax.axis_index("rows")
    col = lax.axis_index("cols")
    x = rows // (ZS * YS)
    z = (rows // YS) % ZS
    y = rows % YS
    me = x * YS + y
    chunk = x_own.shape[1]
    every = tops.shape[0]
    share = BLOCK // ZS

    def member(a, b):
        return ((x + a) % XS) * YS + (y + b) % YS

    def source(a, b):
        return ((x + XS - a) % XS) * YS + (y + YS - b) % YS

    def row_of(a, b):
        return (((x + a) % XS) * ZS + z) * YS + (y + b) % YS

    def ring_row(d):
        return (x * ZS + (z + d) % ZS) * YS + y

    after = (col + 1) % CS
    before = (col + CS - 1) % CS

    barrier = pltpu.get_barrier_semaphore()

    def greet(row, column):
        pl.semaphore_signal(barrier, inc=1, device_id=(row, column), device_id_type=MESH)

    for a, b in PEERS:
        greet(row_of(a, b), col)
        greet(row_of(a, b), before)
    greet(rows, before)
    for d in RING:
        greet(ring_row(d), col)

    def remote(src, dst, send, recv, row, column):
        return pltpu.make_async_remote_copy(
            src_ref=src, dst_ref=dst, send_sem=send, recv_sem=recv, device_id=(row, column), device_id_type=MESH
        )

    plan_copy = pltpu.make_async_copy(plan_hbm, plan_ref, load_sem.at[8, 0])
    own_place = pl.ds(pl.multiple_of(me * chunk, chunk), chunk)
    loads = {}
    for half in range(2):
        for k, (a, b) in enumerate(PEERS):
            slot = 2 * member(a, b) + half
            loads[k, half] = pltpu.make_async_copy(x_hbm.at[:, slot, :], x_own.at[slot], load_sem.at[k, half])
        gathered = (tops, bottoms)[half]
        loads[7, half] = pltpu.make_async_copy(x_hbm.at[:, 2 * me + half, :], gathered.at[own_place], load_sem.at[7, half])
    for half in range(2):
        for k in range(8):
            loads[k, half].start()
    plan_copy.start()

    pl.semaphore_wait(barrier, 2 * len(PEERS) + 1 + len(RING))

    incoming = {}
    for half in range(2):
        gathered = (tops, bottoms)[half]
        for k, (a, b) in enumerate(PEERS):
            loads[k, half].wait()
            incoming[k, half] = remote(
                x_own.at[2 * member(a, b) + half],
                gathered.at[own_place],
                in_send.at[k, half],
                in_recv.at[k, half],
                row_of(a, b),
                col,
            )
            incoming[k, half].start()
    plan_copy.wait()
    loads[7, 0].wait()
    loads[7, 1].wait()

    def ring_place(d):
        return pl.ds(pl.multiple_of(((z + d) % ZS) * share, share), share)

    for k in range(len(PEERS)):
        incoming[k, 0].wait_recv()
    top_now = tops[...]
    partial[0] = full_product(top_now, top_now, FIRST)
    sums = {}
    for n, d in enumerate(RING):
        sums[n, 0] = remote(
            partial.at[0, ring_place(d)], shares_tt.at[n], sum_send.at[n, 0], sum_recv.at[n, 0], ring_row(d), col
        )
        sums[n, 0].start()

    for k in range(len(PEERS)):
        incoming[k, 1].wait_recv()
    bottom_now = bottoms[...]
    partial[1] = full_product(top_now, bottom_now, FIRST)
    partial[2] = full_product(bottom_now, bottom_now, FIRST)
    for n, d in enumerate(RING):
        sums[n, 1] = remote(
            partial.at[1:3, ring_place(d)], shares_b.at[n], sum_send.at[n, 1], sum_recv.at[n, 1], ring_row(d), col
        )
        sums[n, 1].start()

    spread = {}
    here = ring_place(0)
    for n in range(len(RING)):
        sums[n, 0].wait_recv()
    mine = partial[0, here]
    for n in range(len(RING)):
        mine = mine + shares_tt[n]
    total_mine[0] = mine
    total[0, here] = mine
    for n, d in enumerate(RING):
        spread[n, 0] = remote(
            total_mine.at[0], total.at[0, here], all_send.at[n, 0], all_recv.at[n, 0], ring_row(d), col
        )
        spread[n, 0].start()
    for n in range(len(RING)):
        sums[n, 1].wait_recv()
    mine = partial[1:3, here]
    for n in range(len(RING)):
        mine = mine + shares_b[n]
    total_mine[1:3] = mine
    total[1:3, here] = mine
    for n, d in enumerate(RING):
        spread[n, 1] = remote(
            total_mine.at[1:3], total.at[1:3, here], all_send.at[n, 1], all_recv.at[n, 1], ring_row(d), col
        )
        spread[n, 1].start()
    for n in range(len(RING)):
        spread[n, 0].wait_recv()
        spread[n, 1].wait_recv()

    cross = total[1]
    gram = jnp.concatenate(
        [jnp.concatenate([total[0], cross], axis=1), jnp.concatenate([jnp.transpose(cross), total[2]], axis=1)], axis=0
    )
    rounds = plan_ref.shape[1]
    gram, rotation = solve(gram, lambda r: plan_ref[0, r : r + 1, :], rounds, True)
    top_square = gram[:BLOCK, :BLOCK]
    square_out[...] = gram[BLOCK:, BLOCK:]
    square = remote(square_out, square_in, next_send.at[0], next_recv.at[0], rows, after)
    square.start()
    pieces = 4
    piece = every // pieces
    moves = []
    for n in range(pieces):
        place = pl.ds(n * piece, piece)
        now = full_product(jnp.concatenate([tops[place], bottoms[place]], axis=1), rotation)
        tops_now[place] = now[:, :BLOCK]
        bottoms_out[place] = now[:, BLOCK:]
        move = remote(
            bottoms_out.at[place], bottoms_in.at[place], next_send.at[1 + n], next_recv.at[1 + n], rows, after
        )
        move.start()
        moves.append(move)

    square.wait_recv()
    cross = jnp.zeros((BLOCK, BLOCK), jnp.float32)
    for n in range(pieces):
        place = pl.ds(n * piece, piece)
        moves[n].wait_recv()
        cross = cross + full_product(tops_now[place], bottoms_in[place], FIRST)
    partial_tb[...] = cross
    sums2 = []
    for n, d in enumerate(RING):
        copy = remote(partial_tb.at[ring_place(d)], shares_tb.at[n], sum2_send.at[n], sum2_recv.at[n], ring_row(d), col)
        copy.start()
        sums2.append(copy)
    for copy in sums2:
        copy.wait_recv()
    mine = partial_tb[here]
    for n in range(len(RING)):
        mine = mine + shares_tb[n]
    total_tb_mine[...] = mine
    total_tb[here] = mine
    spread2 = []
    for n, d in enumerate(RING):
        copy = remote(total_tb_mine, total_tb.at[here], all2_send.at[n], all2_recv.at[n], ring_row(d), col)
        copy.start()
        spread2.append(copy)
    for copy in spread2:
        copy.wait_recv()
    cross = total_tb[...]
    gram = jnp.concatenate(
        [jnp.concatenate([top_square, cross], axis=1), jnp.concatenate([jnp.transpose(cross), square_in[...]], axis=1)],
        axis=0,
    )
    _, rotation = solve(gram, lambda r: plan_ref[1, r : r + 1, :], rounds, False)

    outgoing = {}
    stores = []
    for k, (a, b) in enumerate(PEERS + ((0, 0),)):
        target = member(a, b)
        place = pl.ds(pl.multiple_of(target * chunk, chunk), chunk)
        now = full_product(jnp.concatenate([tops_now[place], bottoms_in[place]], axis=1), rotation)
        result_out[k, 0] = now[:, :BLOCK]
        result_out[k, 1] = now[:, BLOCK:]
        outgoing[k, 1] = remote(
            result_out.at[k, 1], result_in.at[2 * me + 1], out_send.at[k, 1], out_recv.at[k, 1], row_of(a, b), after
        )
        outgoing[k, 1].start()
        if k < len(PEERS):
            outgoing[k, 0] = remote(
                result_out.at[k, 0], result_in.at[2 * me], out_send.at[k, 0], out_recv.at[k, 0], row_of(a, b), col
            )
            outgoing[k, 0].start()
        else:
            store = pltpu.make_async_copy(result_out.at[k, 0], out_hbm.at[:, 2 * me, :], store_sem.at[k, 0])
            store.start()
            stores.append(store)
    for k, (a, b) in enumerate(PEERS + ((0, 0),)):
        for half in (1, 0):
            if (k, half) not in outgoing:
                continue
            outgoing[k, half].wait_recv()
            slot = 2 * source(a, b) + half
            store = pltpu.make_async_copy(result_in.at[slot], out_hbm.at[:, slot, :], store_sem.at[k, half])
            store.start()
            stores.append(store)

    for copies in (incoming, sums, spread, outgoing):
        for copy in copies.values():
            copy.wait_send()
    for copy in [square, *moves, *sums2, *spread2]:
        copy.wait_send()
    for store in stores:
        store.wait()


def body(matrix, plan):
    chunk, pairs, halves, width = matrix.shape
    slots = pairs * halves
    every = chunk * GROUP
    share = BLOCK // ZS
    f32 = jnp.float32
    dma = pltpu.SemaphoreType.DMA
    near, ring = len(PEERS), len(RING)
    vmem = pltpu.VMEM
    result = pl.pallas_call(
        kernel,
        out_shape=jax.ShapeDtypeStruct((chunk, slots, width), f32),
        in_specs=[pl.BlockSpec(memory_space=pl.ANY)] * 2,
        out_specs=pl.BlockSpec(memory_space=pl.ANY),
        scratch_shapes=[
            vmem(plan.shape, jnp.int32),
            vmem((slots, chunk, width), f32),
            vmem((every, width), f32),
            vmem((every, width), f32),
            vmem((3, BLOCK, BLOCK), f32),
            vmem((ring, share, BLOCK), f32),
            vmem((ring, 2, share, BLOCK), f32),
            vmem((3, BLOCK, BLOCK), f32),
            vmem((3, share, BLOCK), f32),
            vmem((every, width), f32),
            vmem((every, width), f32),
            vmem((BLOCK, BLOCK), f32),
            vmem((BLOCK, BLOCK), f32),
            vmem((every, width), f32),
            vmem((BLOCK, BLOCK), f32),
            vmem((ring, share, BLOCK), f32),
            vmem((BLOCK, BLOCK), f32),
            vmem((share, BLOCK), f32),
            vmem((near + 1, 2, chunk, width), f32),
            vmem((slots, chunk, width), f32),
            dma((9, 2)),
            dma((near, 2)),
            dma((near, 2)),
            dma((ring, 2)),
            dma((ring, 2)),
            dma((ring, 2)),
            dma((ring, 2)),
            dma((5,)),
            dma((5,)),
            dma((ring,)),
            dma((ring,)),
            dma((ring,)),
            dma((ring,)),
            dma((near + 1, 2)),
            dma((near + 1, 2)),
            dma((near + 1, 2)),
        ],
        compiler_params=pltpu.CompilerParams(collective_id=0, has_side_effects=True),
        cost_estimate=pl.CostEstimate(flops=10**9, bytes_accessed=2 * matrix.size * 4, transcendentals=0),
        name="jacobi_steps",
    )(matrix.reshape(chunk, slots, width), plan)
    return result.reshape(matrix.shape)


def solution(mesh):
    in_specs = (P("rows", "cols", None, None), P())
    out_specs = P("rows", "cols", None, None)
    return jax.shard_map(body, mesh=mesh, in_specs=in_specs, out_specs=out_specs, check_vma=False)
```

time: 522 us -> 58.9 us (0.11); the launches traced: 515 us -> 58.7 us
  local copies, waits for them, and re-layouts: 170 us -> 1.87 us
  blocking collectives: 122 us -> 0 us
  matrix products: 80.2 us -> 0 us
  waiting for transfers between devices: 79.8 us -> 0 us
  Pallas kernels: 0 us -> 56.9 us
  starting transfers between devices: 44.2 us -> 0 us
  other arithmetic: 17.6 us -> 0 us
    all_to_all x4 -> x0, blocking collectives: 122 us -> none  [the longest x2 64.9 us: summed_rows(): return jnp.sum(lax.all_to_all(own, far, 0, 0, tiled=True), axis=0)]
    dot_general x6 -> x0, local copies, waits for them, and re-layouts: 99.4 us -> none  [diagonalize(): jnp.einsum('pji,pjk->pik', rot_now, product, precision=lax.Precision.HIGH...]
    dot_general x32 -> x0, matrix products: 80.2 us -> none  [the longest x6 25.3 us: diagonalize(): jnp.einsum('pij,pjk->pik', grams, rot_now, precision=lax.Precision.HIGHEST)]
    all_to_all x4 -> x0, waiting for transfers between devices: 73.1 us -> none  [sent_to_all(): return lax.all_to_all(copies, axis, split_axis=0, concat_axis=0, tiled=True)]
    pallas_call x0 -> x1, Pallas kernels: none -> 56.9 us  [body(): pl.pallas_call(kernel, out_shape=jax.ShapeDtypeStruct((chunk, slots, widt...]
    another operation x4 -> x0, local copies, waits for them, and re-layouts: 33.1 us -> none  [the longest x2 32.6 us: total_of(): return lax.slice_in_dim(whole, 0, len(lines)).reshape(value.shape)]
    all_to_all x4 -> x0, starting transfers between devices: 26.3 us -> none  [sent_to_all(): return lax.all_to_all(copies, axis, split_axis=0, concat_axis=0, tiled=True)]
    gather x16 -> x0, local copies, waits for them, and re-layouts: 20.9 us -> none  [diagonalize(): diagonal_now = jnp.diagonal(grams, axis1=1, axis2=2)]
  transfers between devices with their start and end apart: 6 -> 0, of which waited for: 6 -> 0; matrix products, arithmetic and copies ran while one was open for 2% -> 0% of each run, Pallas kernels for 0% -> 0%
where the time goes in v1:
time: 58.9 us; the launch traced here: 58.7 us
  Pallas kernels  56.9 us (97%)
  local copies, waits for them, and re-layouts  1.87 us (3%)
    pallas_call x1, Pallas kernels, body(): pl.pallas_call(kernel, out_shape=jax.ShapeDtypeStruct((chunk, slots, widt...  56.9 us
    unnamed x1, local copies, waits for them, and re-layouts  1.87 us

profile of v1, /device:TPU:1, one launch (start us, length us, event | category | flops | bytes accessed | tf_op | source)
XLA Modules:
  0.0 58.7 jit_solution(6383185533611486019)
XLA Ops:
  0.0 56.9 %jacobi_steps.1 = f32[64,16,128]{2,1,0:T(8,128)} custom-call(f32[64,16,128]{2,1,0:T(8,128)} %bitcast.3, s32[2,4,256]{2,1,0:T(4,128)} %plan_hbm.1), custom_call_target="tpu_custom_call" | custom-call | flops 1000000000 | bytes 1048576 | tf_op jit(solution)/shard_map/jacobi_steps/pallas_call | solution.py:363
  56.9 1.9 %copy.4 = f32[64,8,2,128]{3,2,1,0:T(2,128)} copy(f32[64,8,2,128]{3,2,1,0:T(2,128)} %bitcast.2) | data formatting | bytes 1048576

commit v2 on v1

v2 whole, which is shorter than its diff:
```python
import functools

import jax
import jax.numpy as jnp
from jax import lax
from jax.experimental import pallas as pl
from jax.experimental.pallas import tpu as pltpu
from jax.sharding import PartitionSpec as P

MESH = pl.DeviceIdType.MESH
XS, ZS, YS, CS = 4, 8, 2, 4
GROUP = XS * YS
BLOCK = 128
WIDTH = 2 * BLOCK
PEERS = ((2, 1), (1, 1), (3, 1), (2, 0), (0, 1), (1, 0), (3, 0))
RING = (4, 3, 5, 2, 6, 1, 7)
FIRST = (((0,), (0,)), ((), ()))
PLAIN = (((1,), (0,)), ((), ()))


def parts_of(value):
    high = value.astype(jnp.bfloat16)
    rest = value - high.astype(jnp.float32)
    middle = rest.astype(jnp.bfloat16)
    low = (rest - middle.astype(jnp.float32)).astype(jnp.bfloat16)
    return high, middle, low


def product(a, b, dims):
    return lax.dot_general(a, b, dims, preferred_element_type=jnp.float32)


def full_product(a, b, dims=PLAIN):
    return lax.dot_general(
        a, b, dims, precision=lax.Precision.HIGHEST, preferred_element_type=jnp.float32
    )


def product_of(a, b, dims=PLAIN):
    high = product(a[0], b[0], dims)
    return high + (product(a[0], b[1], dims) + product(a[1], b[0], dims))


def columns_moved(value, partner):
    rows = value.shape[0]
    near = jnp.where(partner < BLOCK, partner, partner - BLOCK)
    sides = []
    for half in range(2):
        lanes = slice(half * BLOCK, (half + 1) * BLOCK)
        index = jnp.broadcast_to(near[:, lanes], (rows, BLOCK))
        left = jnp.broadcast_to(partner[:, lanes] < BLOCK, (rows, BLOCK))
        picked = [
            jnp.take_along_axis(value[:, n * BLOCK : (n + 1) * BLOCK], index, axis=1, mode="promise_in_bounds")
            for n in range(2)
        ]
        sides.append(jnp.where(left, picked[0], picked[1]))
    return jnp.concatenate(sides, axis=1)


def solve(gram, plan_of_round, rounds, final_gram):
    below = lax.broadcasted_iota(jnp.int32, (WIDTH, WIDTH), 0)
    along = lax.broadcasted_iota(jnp.int32, (WIDTH, WIDTH), 1)
    unit = below == along
    block_unit = unit[:BLOCK, :BLOCK]
    index = lax.broadcasted_iota(jnp.int32, (1, WIDTH), 1)
    rotation = None
    for r in range(rounds):
        partner = plan_of_round(r)
        pairing = below == partner
        moved = columns_moved(gram, partner)
        own = jnp.concatenate(
            [
                jnp.sum(jnp.where(block_unit, gram[:BLOCK, :BLOCK], 0.0), axis=0, keepdims=True),
                jnp.sum(jnp.where(block_unit, gram[BLOCK:, BLOCK:], 0.0), axis=0, keepdims=True),
            ],
            axis=1,
        )
        cross = jnp.sum(jnp.where(pairing, gram, 0.0), axis=0, keepdims=True)
        other = columns_moved(jnp.broadcast_to(own, (8, WIDTH)), partner)[:1]
        orient = jnp.where(index < partner, 1.0, -1.0)
        spread = orient * (other - own)
        sign = jnp.where(spread >= 0.0, 1.0, -1.0)
        tangent = sign * 2.0 * cross / (jnp.abs(spread) + jnp.sqrt(spread * spread + 4.0 * cross * cross))
        cosine = 1.0 / jnp.sqrt(1.0 + tangent * tangent)
        sine = -orient * (tangent * cosine)
        if r + 1 < rounds or final_gram:
            turned = jnp.transpose(gram * cosine + moved * sine)
            gram = turned * cosine + columns_moved(turned, partner) * sine
        if rotation is None:
            rotation = jnp.where(unit, cosine, 0.0) + jnp.where(pairing, sine, 0.0)
        else:
            rotation = rotation * cosine + columns_moved(rotation, partner) * sine
    return gram, rotation


def kernel(
    x_hbm,
    plan_hbm,
    result,
    plan_ref,
    x_own,
    tops,
    bottoms,
    partial,
    shares_tt,
    shares_b,
    total,
    total_mine,
    bottoms_out,
    bottoms_in,
    square_out,
    square_in,
    tops_now,
    partial_tb,
    shares_tb,
    total_tb,
    total_tb_mine,
    result_out,
    load_sem,
    in_send,
    in_recv,
    sum_send,
    sum_recv,
    all_send,
    all_recv,
    next_send,
    next_recv,
    sum2_send,
    sum2_recv,
    all2_send,
    all2_recv,
    out_send,
    out_recv,
):
    rows = lax.axis_index("rows")
    col = lax.axis_index("cols")
    x = rows // (ZS * YS)
    z = (rows // YS) % ZS
    y = rows % YS
    me = x * YS + y
    chunk = x_own.shape[1]
    every = tops.shape[0]
    share = BLOCK // ZS
    near, ring = len(PEERS), len(RING)

    def member(a, b):
        return ((x + a) % XS) * YS + (y + b) % YS

    def row_of(a, b):
        return (((x + a) % XS) * ZS + z) * YS + (y + b) % YS

    def ring_row(d):
        return (x * ZS + (z + d) % ZS) * YS + y

    after = (col + 1) % CS
    before = (col + CS - 1) % CS

    def send(src, dst, send_sem, recv_sem, row, column):
        pltpu.make_async_remote_copy(
            src_ref=src, dst_ref=dst, send_sem=send_sem, recv_sem=recv_sem, device_id=(row, column), device_id_type=MESH
        ).start()

    def await_bytes(like, sem):
        pltpu.make_async_remote_copy(
            src_ref=like, dst_ref=like, send_sem=sem, recv_sem=sem, device_id=(rows, col), device_id_type=MESH
        ).wait_recv()

    barrier = pltpu.get_barrier_semaphore()

    def greet(row, column):
        pl.semaphore_signal(barrier, inc=1, device_id=(row, column), device_id_type=MESH)

    for a, b in PEERS:
        greet(row_of(a, b), col)
        greet(row_of(a, b), before)
    greet(rows, before)
    for d in RING:
        greet(ring_row(d), col)

    own_place = pl.ds(pl.multiple_of(me * chunk, chunk), chunk)
    loads = ([], [])
    for half in range(2):
        for a, b in PEERS:
            slot = 2 * member(a, b) + half
            loads[half].append(pltpu.make_async_copy(x_hbm.at[:, slot, :], x_own.at[slot], load_sem.at[half]))
        gathered = (tops, bottoms)[half]
        loads[half].append(pltpu.make_async_copy(x_hbm.at[:, 2 * me + half, :], gathered.at[own_place], load_sem.at[half]))
        for load in loads[half]:
            load.start()
    plan_copy = pltpu.make_async_copy(plan_hbm, plan_ref, load_sem.at[2])
    plan_copy.start()

    pl.semaphore_wait(barrier, 2 * near + 1 + ring)

    for half in range(2):
        gathered = (tops, bottoms)[half]
        for load in loads[half]:
            load.wait()
        for a, b in PEERS:
            send(
                x_own.at[2 * member(a, b) + half],
                gathered.at[own_place],
                in_send,
                in_recv.at[half],
                row_of(a, b),
                col,
            )
    plan_copy.wait()

    def ring_place(d):
        return pl.ds(pl.multiple_of(((z + d) % ZS) * share, share), share)

    await_bytes(tops.at[: near * chunk], in_recv.at[0])
    top_now = tops[...]
    partial[0] = full_product(top_now, top_now, FIRST)
    for n, d in enumerate(RING):
        send(partial.at[0, ring_place(d)], shares_tt.at[n], sum_send, sum_recv.at[0], ring_row(d), col)

    await_bytes(bottoms.at[: near * chunk], in_recv.at[1])
    bottom_now = bottoms[...]
    partial[1] = full_product(top_now, bottom_now, FIRST)
    partial[2] = full_product(bottom_now, bottom_now, FIRST)
    for n, d in enumerate(RING):
        send(partial.at[1:3, ring_place(d)], shares_b.at[n], sum_send, sum_recv.at[1], ring_row(d), col)

    here = ring_place(0)
    await_bytes(shares_tt, sum_recv.at[0])
    mine = partial[0, here]
    for n in range(ring):
        mine = mine + shares_tt[n]
    total_mine[0] = mine
    total[0, here] = mine
    for d in RING:
        send(total_mine.at[0], total.at[0, here], all_send, all_recv.at[0], ring_row(d), col)
    await_bytes(shares_b, sum_recv.at[1])
    mine = partial[1:3, here]
    for n in range(ring):
        mine = mine + shares_b[n]
    total_mine[1:3] = mine
    total[1:3, here] = mine
    for d in RING:
        send(total_mine.at[1:3], total.at[1:3, here], all_send, all_recv.at[1], ring_row(d), col)
    await_bytes(total.at[0, : ring * share], all_recv.at[0])
    await_bytes(total.at[1:3, : ring * share], all_recv.at[1])

    cross = total[1]
    gram = jnp.concatenate(
        [jnp.concatenate([total[0], cross], axis=1), jnp.concatenate([jnp.transpose(cross), total[2]], axis=1)], axis=0
    )
    rounds = plan_ref.shape[1]
    gram, rotation = solve(gram, lambda r: plan_ref[0, r : r + 1, :], rounds, True)
    top_square = gram[:BLOCK, :BLOCK]
    square_out[...] = gram[BLOCK:, BLOCK:]
    send(square_out, square_in, next_send, next_recv.at[0], rows, after)
    pieces = 4
    piece = every // pieces
    columns = parts_of(jnp.concatenate([tops[...], bottoms[...]], axis=1))
    turn = parts_of(rotation)
    for n in range(pieces):
        place = pl.ds(n * piece, piece)
        lines = slice(n * piece, (n + 1) * piece)
        bottoms_out[place] = product_of([part[lines] for part in columns], [part[:, BLOCK:] for part in turn])
        send(bottoms_out.at[place], bottoms_in.at[place], next_send, next_recv.at[1 + n], rows, after)
    tops_now[...] = product_of(columns, [part[:, :BLOCK] for part in turn])

    await_bytes(square_in, next_recv.at[0])
    cross = jnp.zeros((BLOCK, BLOCK), jnp.float32)
    for n in range(pieces):
        place = pl.ds(n * piece, piece)
        await_bytes(bottoms_in.at[place], next_recv.at[1 + n])
        cross = cross + product_of(parts_of(tops_now[place]), parts_of(bottoms_in[place]), FIRST)
    partial_tb[...] = cross
    for n, d in enumerate(RING):
        send(partial_tb.at[ring_place(d)], shares_tb.at[n], sum2_send, sum2_recv, ring_row(d), col)
    await_bytes(shares_tb, sum2_recv)
    mine = partial_tb[here]
    for n in range(ring):
        mine = mine + shares_tb[n]
    total_tb_mine[...] = mine
    total_tb[here] = mine
    for d in RING:
        send(total_tb_mine, total_tb.at[here], all2_send, all2_recv, ring_row(d), col)
    await_bytes(total_tb.at[: ring * share], all2_recv)
    cross = total_tb[...]
    gram = jnp.concatenate(
        [jnp.concatenate([top_square, cross], axis=1), jnp.concatenate([jnp.transpose(cross), square_in[...]], axis=1)],
        axis=0,
    )
    _, rotation = solve(gram, lambda r: plan_ref[1, r : r + 1, :], rounds, False)

    turn = parts_of(rotation)
    for k, (a, b) in enumerate(PEERS + ((0, 0),)):
        place = pl.ds(pl.multiple_of(member(a, b) * chunk, chunk), chunk)
        now = product_of(parts_of(jnp.concatenate([tops_now[place], bottoms_in[place]], axis=1)), turn)
        result_out[k, 1] = now[:, BLOCK:]
        send(result_out.at[k, 1], result.at[2 * me + 1], out_send, out_recv, row_of(a, b), after)
        if k < near:
            result_out[k, 0] = now[:, :BLOCK]
            send(result_out.at[k, 0], result.at[2 * me], out_send, out_recv, row_of(a, b), col)
        else:
            result[2 * me] = now[:, :BLOCK]
    await_bytes(result.at[: 2 * near + 1], out_recv)
    await_bytes(x_own.at[: 2 * near], in_send)
    await_bytes(tops.at[: 3 * ring * share], sum_send)
    await_bytes(tops.at[: 3 * ring * share], all_send)
    await_bytes(tops, next_send)
    await_bytes(square_out, next_send)
    await_bytes(shares_tb, sum2_send)
    await_bytes(shares_tb, all2_send)
    await_bytes(result.at[: 2 * near + 1], out_send)


def body(matrix, plan):
    chunk, pairs, halves, width = matrix.shape
    slots = pairs * halves
    every = chunk * GROUP
    share = BLOCK // ZS
    f32 = jnp.float32
    dma = pltpu.SemaphoreType.DMA
    near, ring = len(PEERS), len(RING)
    vmem = pltpu.VMEM
    result = pl.pallas_call(
        kernel,
        out_shape=jax.ShapeDtypeStruct((slots, chunk, width), f32),
        in_specs=[pl.BlockSpec(memory_space=pltpu.HBM)] * 2,
        out_specs=pl.BlockSpec(memory_space=pltpu.VMEM),
        scratch_shapes=[
            vmem(plan.shape, jnp.int32),
            vmem((slots, chunk, width), f32),
            vmem((every, width), f32),
            vmem((every, width), f32),
            vmem((3, BLOCK, BLOCK), f32),
            vmem((ring, share, BLOCK), f32),
            vmem((ring, 2, share, BLOCK), f32),
            vmem((3, BLOCK, BLOCK), f32),
            vmem((3, share, BLOCK), f32),
            vmem((every, width), f32),
            vmem((every, width), f32),
            vmem((BLOCK, BLOCK), f32),
            vmem((BLOCK, BLOCK), f32),
            vmem((every, width), f32),
            vmem((BLOCK, BLOCK), f32),
            vmem((ring, share, BLOCK), f32),
            vmem((BLOCK, BLOCK), f32),
            vmem((share, BLOCK), f32),
            vmem((near + 1, 2, chunk, width), f32),
            dma((3,)),
            dma,
            dma((2,)),
            dma,
            dma((2,)),
            dma,
            dma((2,)),
            dma,
            dma((5,)),
            dma,
            dma,
            dma,
            dma,
            dma,
            dma,
        ],
        compiler_params=pltpu.CompilerParams(collective_id=0, has_side_effects=True, vmem_limit_bytes=24 * 2**20),
        cost_estimate=pl.CostEstimate(flops=10**9, bytes_accessed=2 * matrix.size * 4, transcendentals=0),
        name="jacobi_steps",
    )(matrix.reshape(chunk, slots, width), plan)
    return result.transpose(1, 0, 2).reshape(matrix.shape)


def solution(mesh):
    in_specs = (P("rows", "cols", None, None), P())
    out_specs = P("rows", "cols", None, None)
    return jax.shard_map(body, mesh=mesh, in_specs=in_specs, out_specs=out_specs, check_vma=False)
```

time: 58.9 us -> 56.8 us (0.964)
  Pallas kernels: 56.9 us -> 53.7 us
  local copies, waits for them, and re-layouts: 1.87 us -> 2.94 us
    pallas_call x1, Pallas kernels: 56.9 us -> 53.7 us  [body(): pl.pallas_call(kernel, out_shape=jax.ShapeDtypeStruct((slots, chunk, widt...]
    reshape x0 -> x1, local copies, waits for them, and re-layouts: none -> 1.2 us  [body(): return result.transpose(1, 0, 2).reshape(matrix.shape)]
    unnamed x1 -> x4, local copies, waits for them, and re-layouts: 1.87 us -> 1.74 us
where the time goes in v2:
time: 56.8 us; the launch traced here: 56.6 us
  Pallas kernels  53.7 us (95%)
  local copies, waits for them, and re-layouts  2.94 us (5%)
    pallas_call x1, Pallas kernels, body(): pl.pallas_call(kernel, out_shape=jax.ShapeDtypeStruct((slots, chunk, widt...  53.7 us
    unnamed x4, local copies, waits for them, and re-layouts  1.74 us
    reshape x1, local copies, waits for them, and re-layouts, body(): return result.transpose(1, 0, 2).reshape(matrix.shape)  1.2 us

profile of v2, /device:TPU:1, one launch (start us, length us, event | category | flops | bytes accessed | tf_op | source)
XLA Modules:
  0.0 56.6 jit_solution(6664185706024980887)
XLA Ops:
  0.0 0.0 copy-start
  0.0 1.0 %copy-done = f32[64,8,2,128]{3,2,1,0:T(2,128)S(1)} copy-done((f32[64,8,2,128]{3,2,1,0:T(2,128)S(1)}, f32[64,8,2,128]{3,2,1,0:T(2,128)}, u32[]{:S(2)}) %copy-start) | copy-done | bytes 524312
  1.0 0.0 copy-start.1
  1.0 0.7 %copy-done.1 = s32[2,4,256]{2,1,0:T(4,128)S(1)} copy-done((s32[2,4,256]{2,1,0:T(4,128)S(1)}, s32[2,4,256]{2,1,0:T(4,128)}, u32[]{:S(2)}) %copy-start.1) | copy-done | bytes 8216
  1.7 53.7 %jacobi_steps.1 = f32[16,64,128]{2,1,0:T(8,128)S(1)} custom-call(f32[64,16,128]{2,1,0:T(8,128)S(1)} %bitcast.5, s32[2,4,256]{2,1,0:T(4,128)S(1)} %copy-done.1), custom_call_target="tpu_custom_call" | custom-call | flops 1000000000 | bytes 1048576 | tf_op jit(solution)/shard_map/jacobi_steps/pallas_call | solution.py:322
  55.5 1.2 %copy.3 = f32[64,8,2,128]{3,2,1,0:T(2,128)} copy(f32[64,8,2,128]{3,0,2,1:T(8,128)S(1)} %bitcast.4) | data formatting | bytes 1048576 | tf_op jit(solution)/shard_map/reshape | solution.py:367
Async XLA Ops:
  0.0 1.0 %copy-start = (f32[64,8,2,128]{3,2,1,0:T(2,128)S(1)}, f32[64,8,2,128]{3,2,1,0:T(2,128)}, u32[]{:S(2)}) copy-start(f32[64,8,2,128]{3,2,1,0:T(2,128)} %param.2) | copy-start | bytes 1572868
  1.0 0.7 %copy-start.1 = (s32[2,4,256]{2,1,0:T(4,128)S(1)}, s32[2,4,256]{2,1,0:T(4,128)}, u32[]{:S(2)}) copy-start(s32[2,4,256]{2,1,0:T(4,128)} %plan_hbm.1) | copy-start | bytes 24580

commit v3 on v2

--- a/solution.py
+++ b/solution.py
@@ -39,6 +39,21 @@
 def product_of(a, b, dims=PLAIN):
     high = product(a[0], b[0], dims)
     return high + (product(a[0], b[1], dims) + product(a[1], b[0], dims))
+
+
+def times_onehot(value, partner):
+    rows = lax.broadcasted_iota(jnp.int32, (WIDTH, WIDTH), 0)
+    onehot = (rows == partner).astype(jnp.float32).astype(jnp.bfloat16)
+    high, middle, low = parts_of(value)
+    return product(high, onehot, PLAIN) + (product(middle, onehot, PLAIN) + product(low, onehot, PLAIN))
+
+
+def turned_by(rotation, partner, cosine, sine):
+    if rotation is None:
+        below = lax.broadcasted_iota(jnp.int32, (WIDTH, WIDTH), 0)
+        along = lax.broadcasted_iota(jnp.int32, (WIDTH, WIDTH), 1)
+        return jnp.where(below == along, cosine, 0.0) + jnp.where(below == partner, sine, 0.0)
+    return rotation * cosine + times_onehot(rotation, partner) * sine
 
 
 def columns_moved(value, partner):
@@ -57,7 +72,7 @@
     return jnp.concatenate(sides, axis=1)
 
 
-def solve(gram, plan_of_round, rounds, final_gram):
+def solve(gram, plan_of_round, rounds, final_gram, tell):
     below = lax.broadcasted_iota(jnp.int32, (WIDTH, WIDTH), 0)
     along = lax.broadcasted_iota(jnp.int32, (WIDTH, WIDTH), 1)
     unit = below == along
@@ -83,13 +98,11 @@
         tangent = sign * 2.0 * cross / (jnp.abs(spread) + jnp.sqrt(spread * spread + 4.0 * cross * cross))
         cosine = 1.0 / jnp.sqrt(1.0 + tangent * tangent)
         sine = -orient * (tangent * cosine)
+        tell(r, cosine, sine)
         if r + 1 < rounds or final_gram:
             turned = jnp.transpose(gram * cosine + moved * sine)
             gram = turned * cosine + columns_moved(turned, partner) * sine
-        if rotation is None:
-            rotation = jnp.where(unit, cosine, 0.0) + jnp.where(pairing, sine, 0.0)
-        else:
-            rotation = rotation * cosine + columns_moved(rotation, partner) * sine
+        rotation = turned_by(rotation, partner, cosine, sine)
     return gram, rotation
 
 
@@ -106,7 +119,10 @@
     shares_b,
     total,
     total_mine,
-    bottoms_out,
+    next_tops,
+    next_bottoms,
+    turns_out,
+    turns_in,
     bottoms_in,
     square_out,
     square_in,
@@ -218,10 +234,14 @@
 
     await_bytes(bottoms.at[: near * chunk], in_recv.at[1])
     bottom_now = bottoms[...]
-    partial[1] = full_product(top_now, bottom_now, FIRST)
-    partial[2] = full_product(bottom_now, bottom_now, FIRST)
+    both = full_product(bottom_now, jnp.concatenate([top_now, bottom_now], axis=1), FIRST)
+    partial[1] = both[:, :BLOCK]
+    partial[2] = both[:, BLOCK:]
     for n, d in enumerate(RING):
         send(partial.at[1:3, ring_place(d)], shares_b.at[n], sum_send, sum_recv.at[1], ring_row(d), col)
+
+    send(tops, next_tops, next_send, next_recv.at[0], rows, after)
+    send(bottoms, next_bottoms, next_send, next_recv.at[1], rows, after)
 
     here = ring_place(0)
     await_bytes(shares_tt, sum_recv.at[0])
@@ -240,38 +260,46 @@
     total[1:3, here] = mine
     for d in RING:
         send(total_mine.at[1:3], total.at[1:3, here], all_send, all_recv.at[1], ring_row(d), col)
+    await_bytes(next_tops, next_recv.at[0])
+    await_bytes(next_bottoms, next_recv.at[1])
+    columns = parts_of(jnp.concatenate([top_now, bottom_now], axis=1))
+    next_columns = parts_of(jnp.concatenate([next_tops[...], next_bottoms[...]], axis=1))
+    between = product_of(columns, next_columns, FIRST)
     await_bytes(total.at[0, : ring * share], all_recv.at[0])
     await_bytes(total.at[1:3, : ring * share], all_recv.at[1])
 
     cross = total[1]
     gram = jnp.concatenate(
-        [jnp.concatenate([total[0], cross], axis=1), jnp.concatenate([jnp.transpose(cross), total[2]], axis=1)], axis=0
+        [jnp.concatenate([total[0], jnp.transpose(cross)], axis=1), jnp.concatenate([cross, total[2]], axis=1)], axis=0
     )
     rounds = plan_ref.shape[1]
-    gram, rotation = solve(gram, lambda r: plan_ref[0, r : r + 1, :], rounds, True)
+
+    def first_plan(r):
+        return plan_ref[0, r : r + 1, :]
+
+    def tell(r, cosine, sine):
+        turns_out[r] = jnp.concatenate([cosine, sine], axis=0)
+        send(turns_out.at[r], turns_in.at[r], next_send, next_recv.at[2 + r], rows, after)
+
+    gram, rotation = solve(gram, first_plan, rounds, True, tell)
     top_square = gram[:BLOCK, :BLOCK]
     square_out[...] = gram[BLOCK:, BLOCK:]
-    send(square_out, square_in, next_send, next_recv.at[0], rows, after)
-    pieces = 4
-    piece = every // pieces
-    columns = parts_of(jnp.concatenate([tops[...], bottoms[...]], axis=1))
-    turn = parts_of(rotation)
-    for n in range(pieces):
-        place = pl.ds(n * piece, piece)
-        lines = slice(n * piece, (n + 1) * piece)
-        bottoms_out[place] = product_of([part[lines] for part in columns], [part[:, BLOCK:] for part in turn])
-        send(bottoms_out.at[place], bottoms_in.at[place], next_send, next_recv.at[1 + n], rows, after)
-    tops_now[...] = product_of(columns, [part[:, :BLOCK] for part in turn])
-
-    await_bytes(square_in, next_recv.at[0])
-    cross = jnp.zeros((BLOCK, BLOCK), jnp.float32)
-    for n in range(pieces):
-        place = pl.ds(n * piece, piece)
-        await_bytes(bottoms_in.at[place], next_recv.at[1 + n])
-        cross = cross + product_of(parts_of(tops_now[place]), parts_of(bottoms_in[place]), FIRST)
-    partial_tb[...] = cross
+    send(square_out, square_in, next_send, next_recv.at[2 + rounds], rows, after)
+
+    turns = []
+    for r in range(rounds):
+        moved = columns_moved(between, first_plan(r))
+        await_bytes(turns_in.at[r], next_recv.at[2 + r])
+        turns.append((turns_in[r, 0:1, :], turns_in[r, 1:2, :]))
+        between = between * turns[r][0] + moved * turns[r][1]
+    partial_tb[...] = full_product(rotation[:, :BLOCK], between[:, BLOCK:], FIRST)
     for n, d in enumerate(RING):
         send(partial_tb.at[ring_place(d)], shares_tb.at[n], sum2_send, sum2_recv, ring_row(d), col)
+    next_rotation = None
+    for r in range(rounds):
+        next_rotation = turned_by(next_rotation, first_plan(r), *turns[r])
+    bottoms_in[...] = product_of(next_columns, [part[:, BLOCK:] for part in parts_of(next_rotation)])
+    tops_now[...] = product_of(columns, [part[:, :BLOCK] for part in parts_of(rotation)])
     await_bytes(shares_tb, sum2_recv)
     mine = partial_tb[here]
     for n in range(ring):
@@ -280,13 +308,14 @@
     total_tb[here] = mine
     for d in RING:
         send(total_tb_mine, total_tb.at[here], all2_send, all2_recv, ring_row(d), col)
+    await_bytes(square_in, next_recv.at[2 + rounds])
     await_bytes(total_tb.at[: ring * share], all2_recv)
     cross = total_tb[...]
     gram = jnp.concatenate(
         [jnp.concatenate([top_square, cross], axis=1), jnp.concatenate([jnp.transpose(cross), square_in[...]], axis=1)],
         axis=0,
     )
-    _, rotation = solve(gram, lambda r: plan_ref[1, r : r + 1, :], rounds, False)
+    _, rotation = solve(gram, lambda r: plan_ref[1, r : r + 1, :], rounds, False, lambda *_: None)
 
     turn = parts_of(rotation)
     for k, (a, b) in enumerate(PEERS + ((0, 0),)):
@@ -304,6 +333,8 @@
     await_bytes(tops.at[: 3 * ring * share], sum_send)
     await_bytes(tops.at[: 3 * ring * share], all_send)
     await_bytes(tops, next_send)
+    await_bytes(bottoms, next_send)
+    await_bytes(turns_out, next_send)
     await_bytes(square_out, next_send)
     await_bytes(shares_tb, sum2_send)
     await_bytes(shares_tb, all2_send)
@@ -336,6 +367,9 @@
             vmem((3, share, BLOCK), f32),
             vmem((every, width), f32),
             vmem((every, width), f32),
+            vmem((plan.shape[1], 2, WIDTH), f32),
+            vmem((plan.shape[1], 2, WIDTH), f32),
+            vmem((every, width), f32),
             vmem((BLOCK, BLOCK), f32),
             vmem((BLOCK, BLOCK), f32),
             vmem((every, width), f32),
@@ -352,7 +386,7 @@
             dma,
             dma((2,)),
             dma,
-            dma((5,)),
+            dma((7,)),
             dma,
             dma,
             dma,
@@ -363,7 +397,7 @@
         compiler_params=pltpu.CompilerParams(collective_id=0, has_side_effects=True, vmem_limit_bytes=24 * 2**20),
         cost_estimate=pl.CostEstimate(flops=10**9, bytes_accessed=2 * matrix.size * 4, transcendentals=0),
         name="jacobi_steps",
-    )(matrix.reshape(chunk, slots, width), plan)
+    )(pltpu.with_memory_space_constraint(matrix.reshape(chunk, slots, width), pltpu.HBM), pltpu.with_memory_space_constraint(plan, pltpu.HBM))
     return result.transpose(1, 0, 2).reshape(matrix.shape)
 
 

time: 56.8 us -> 53.7 us (0.945)
  local copies, waits for them, and re-layouts: 2.94 us -> 1.2 us
  Pallas kernels: 53.7 us -> 52.4 us
    unnamed x4 -> x0, local copies, waits for them, and re-layouts: 1.74 us -> none
    pallas_call x1, Pallas kernels: 53.7 us -> 52.4 us  [body(): pl.pallas_call(kernel, out_shape=jax.ShapeDtypeStruct((slots, chunk, widt...]
where the time goes in v3:
time: 53.7 us; the launch traced here: 53.6 us
  Pallas kernels  52.4 us (98%)
  local copies, waits for them, and re-layouts  1.2 us (2%)
    pallas_call x1, Pallas kernels, body(): pl.pallas_call(kernel, out_shape=jax.ShapeDtypeStruct((slots, chunk, widt...  52.4 us
    reshape x1, local copies, waits for them, and re-layouts, body(): return result.transpose(1, 0, 2).reshape(matrix.shape)  1.2 us

profile of v3, /device:TPU:1, one launch (start us, length us, event | category | flops | bytes accessed | tf_op | source)
XLA Modules:
  0.0 53.6 jit_solution(17767682158106625491)
XLA Ops:
  0.0 52.4 %jacobi_steps.1 = f32[16,64,128]{2,1,0:T(8,128)S(1)} custom-call(f32[64,16,128]{2,1,0:T(8,128)} %bitcast.5, s32[2,4,256]{2,1,0:T(4,128)} %plan_hbm.1), custom_call_target="tpu_custom_call" | custom-call | flops 1000000000 | bytes 1048576 | tf_op jit(solution)/shard_map/jacobi_steps/pallas_call | solution.py:353
  52.4 1.2 %copy.3 = f32[64,8,2,128]{3,2,1,0:T(2,128)} copy(f32[64,8,2,128]{3,0,2,1:T(8,128)S(1)} %bitcast.4) | data formatting | bytes 1048576 | tf_op jit(solution)/shard_map/reshape | solution.py:401

commit v4 on v3

--- a/solution.py
+++ b/solution.py
@@ -72,38 +72,37 @@
     return jnp.concatenate(sides, axis=1)
 
 
-def solve(gram, plan_of_round, rounds, final_gram, tell):
+def solve(gram, plan_of_round, rounds, tell):
     below = lax.broadcasted_iota(jnp.int32, (WIDTH, WIDTH), 0)
     along = lax.broadcasted_iota(jnp.int32, (WIDTH, WIDTH), 1)
-    unit = below == along
-    block_unit = unit[:BLOCK, :BLOCK]
     index = lax.broadcasted_iota(jnp.int32, (1, WIDTH), 1)
     rotation = None
+    image = gram
     for r in range(rounds):
         partner = plan_of_round(r)
-        pairing = below == partner
-        moved = columns_moved(gram, partner)
-        own = jnp.concatenate(
-            [
-                jnp.sum(jnp.where(block_unit, gram[:BLOCK, :BLOCK], 0.0), axis=0, keepdims=True),
-                jnp.sum(jnp.where(block_unit, gram[BLOCK:, BLOCK:], 0.0), axis=0, keepdims=True),
-            ],
-            axis=1,
-        )
-        cross = jnp.sum(jnp.where(pairing, gram, 0.0), axis=0, keepdims=True)
+        if r == 0:
+            unit = below == along
+            pairing = below == partner
+            own = jnp.sum(jnp.where(unit, gram, 0.0), axis=0, keepdims=True)
+            cross = jnp.sum(jnp.where(pairing, gram, 0.0), axis=0, keepdims=True)
+        else:
+            own = jnp.sum(rotation * image, axis=0, keepdims=True)
+            rotation_moved = columns_moved(rotation, partner)
+            cross = jnp.sum(rotation_moved * image, axis=0, keepdims=True)
         other = columns_moved(jnp.broadcast_to(own, (8, WIDTH)), partner)[:1]
         orient = jnp.where(index < partner, 1.0, -1.0)
         spread = orient * (other - own)
         sign = jnp.where(spread >= 0.0, 1.0, -1.0)
         tangent = sign * 2.0 * cross / (jnp.abs(spread) + jnp.sqrt(spread * spread + 4.0 * cross * cross))
-        cosine = 1.0 / jnp.sqrt(1.0 + tangent * tangent)
+        cosine = lax.rsqrt(1.0 + tangent * tangent)
         sine = -orient * (tangent * cosine)
         tell(r, cosine, sine)
-        if r + 1 < rounds or final_gram:
-            turned = jnp.transpose(gram * cosine + moved * sine)
-            gram = turned * cosine + columns_moved(turned, partner) * sine
-        rotation = turned_by(rotation, partner, cosine, sine)
-    return gram, rotation
+        if r == 0:
+            rotation = jnp.where(unit, cosine, 0.0) + jnp.where(pairing, sine, 0.0)
+        else:
+            rotation = rotation * cosine + rotation_moved * sine
+        image = image * cosine + columns_moved(image, partner) * sine
+    return rotation, image
 
 
 def kernel(
@@ -281,9 +280,9 @@
         turns_out[r] = jnp.concatenate([cosine, sine], axis=0)
         send(turns_out.at[r], turns_in.at[r], next_send, next_recv.at[2 + r], rows, after)
 
-    gram, rotation = solve(gram, first_plan, rounds, True, tell)
-    top_square = gram[:BLOCK, :BLOCK]
-    square_out[...] = gram[BLOCK:, BLOCK:]
+    rotation, image = solve(gram, first_plan, rounds, tell)
+    square_out[...] = full_product(rotation[:, BLOCK:], image[:, BLOCK:], FIRST)
+    top_square = full_product(rotation[:, :BLOCK], image[:, :BLOCK], FIRST)
     send(square_out, square_in, next_send, next_recv.at[2 + rounds], rows, after)
 
     turns = []
@@ -315,7 +314,7 @@
         [jnp.concatenate([top_square, cross], axis=1), jnp.concatenate([jnp.transpose(cross), square_in[...]], axis=1)],
         axis=0,
     )
-    _, rotation = solve(gram, lambda r: plan_ref[1, r : r + 1, :], rounds, False, lambda *_: None)
+    rotation, _ = solve(gram, lambda r: plan_ref[1, r : r + 1, :], rounds, lambda *_: None)
 
     turn = parts_of(rotation)
     for k, (a, b) in enumerate(PEERS + ((0, 0),)):

time: 53.7 us -> 52.6 us (0.980)
  Pallas kernels: 52.4 us -> 51.3 us
    pallas_call x1, Pallas kernels: 52.4 us -> 51.3 us  [body(): pl.pallas_call(kernel, out_shape=jax.ShapeDtypeStruct((slots, chunk, widt...]
where the time goes in v4:
time: 52.6 us; the launch traced here: 52.5 us
  Pallas kernels  51.3 us (98%)
  local copies, waits for them, and re-layouts  1.2 us (2%)
    pallas_call x1, Pallas kernels, body(): pl.pallas_call(kernel, out_shape=jax.ShapeDtypeStruct((slots, chunk, widt...  51.3 us
    reshape x1, local copies, waits for them, and re-layouts, body(): return result.transpose(1, 0, 2).reshape(matrix.shape)  1.2 us

profile of v4, /device:TPU:1, one launch (start us, length us, event | category | flops | bytes accessed | tf_op | source)
XLA Modules:
  0.0 52.5 jit_solution(18435126912172915981)
XLA Ops:
  0.0 51.3 %jacobi_steps.1 = f32[16,64,128]{2,1,0:T(8,128)S(1)} custom-call(f32[64,16,128]{2,1,0:T(8,128)} %bitcast.5, s32[2,4,256]{2,1,0:T(4,128)} %plan_hbm.1), custom_call_target="tpu_custom_call" | custom-call | flops 1000000000 | bytes 1048576 | tf_op jit(solution)/shard_map/jacobi_steps/pallas_call | solution.py:352
  51.3 1.2 %copy.3 = f32[64,8,2,128]{3,2,1,0:T(2,128)} copy(f32[64,8,2,128]{3,0,2,1:T(8,128)S(1)} %bitcast.4) | data formatting | bytes 1048576 | tf_op jit(solution)/shard_map/reshape | solution.py:400

commit v5 on v4

--- a/solution.py
+++ b/solution.py
@@ -12,7 +12,7 @@
 GROUP = XS * YS
 BLOCK = 128
 WIDTH = 2 * BLOCK
-PEERS = ((2, 1), (1, 1), (3, 1), (2, 0), (0, 1), (1, 0), (3, 0))
+PEERS = ((2, 1), (0, 1), (1, 1), (2, 0), (3, 1), (1, 0), (3, 0))
 RING = (4, 3, 5, 2, 6, 1, 7)
 FIRST = (((0,), (0,)), ((), ()))
 PLAIN = (((1,), (0,)), ((), ()))
@@ -167,6 +167,15 @@
     def ring_row(d):
         return (x * ZS + (z + d) % ZS) * YS + y
 
+    lane = col % 2
+    other_lane = 1 - lane
+    base = col - lane
+    adds = lane == 1
+
+    def by_core(adding, plain):
+        pl.when(adds)(adding)
+        pl.when(jnp.logical_not(adds))(plain)
+
     after = (col + 1) % CS
     before = (col + CS - 1) % CS
 
@@ -190,7 +199,9 @@
         greet(row_of(a, b), before)
     greet(rows, before)
     for d in RING:
-        greet(ring_row(d), col)
+        greet(ring_row(d), base)
+        greet(ring_row(d), base + 1)
+    greet(rows, base + other_lane)
 
     own_place = pl.ds(pl.multiple_of(me * chunk, chunk), chunk)
     loads = ([], [])
@@ -205,7 +216,7 @@
     plan_copy = pltpu.make_async_copy(plan_hbm, plan_ref, load_sem.at[2])
     plan_copy.start()
 
-    pl.semaphore_wait(barrier, 2 * near + 1 + ring)
+    pl.semaphore_wait(barrier, 2 * near + 1 + 2 * ring + 1)
 
     for half in range(2):
         gathered = (tops, bottoms)[half]
@@ -225,47 +236,69 @@
     def ring_place(d):
         return pl.ds(pl.multiple_of(((z + d) % ZS) * share, share), share)
 
+    here = ring_place(0)
+
+    def scatter(take, slots, send_sem, recv_sems):
+        for n, d in enumerate(RING):
+            send(take(ring_place(d)), slots.at[lane, n], send_sem, recv_sems.at[lane], ring_row(d), base + 1)
+
+        @pl.when(jnp.logical_not(adds))
+        def _():
+            send(take(here), slots.at[0, ring], send_sem, recv_sems.at[0], rows, base + 1)
+
+    def gather(core, mine, home, send_sem, recv_sem):
+        for d in RING:
+            send(mine, home, send_sem, recv_sem, ring_row(d), base + core)
+        if core == 0:
+            send(mine, home, send_sem, recv_sem, rows, base)
+
     await_bytes(tops.at[: near * chunk], in_recv.at[0])
     top_now = tops[...]
     partial[0] = full_product(top_now, top_now, FIRST)
-    for n, d in enumerate(RING):
-        send(partial.at[0, ring_place(d)], shares_tt.at[n], sum_send, sum_recv.at[0], ring_row(d), col)
+    scatter(lambda place: partial.at[0:1, place], shares_tt, sum_send, sum_recv.at[0])
 
     await_bytes(bottoms.at[: near * chunk], in_recv.at[1])
     bottom_now = bottoms[...]
     both = full_product(bottom_now, jnp.concatenate([top_now, bottom_now], axis=1), FIRST)
     partial[1] = both[:, :BLOCK]
     partial[2] = both[:, BLOCK:]
-    for n, d in enumerate(RING):
-        send(partial.at[1:3, ring_place(d)], shares_b.at[n], sum_send, sum_recv.at[1], ring_row(d), col)
+    scatter(lambda place: partial.at[1:3, place], shares_b, sum_send, sum_recv.at[1])
 
     send(tops, next_tops, next_send, next_recv.at[0], rows, after)
     send(bottoms, next_bottoms, next_send, next_recv.at[1], rows, after)
 
-    here = ring_place(0)
-    await_bytes(shares_tt, sum_recv.at[0])
-    mine = partial[0, here]
-    for n in range(ring):
-        mine = mine + shares_tt[n]
-    total_mine[0] = mine
-    total[0, here] = mine
-    for d in RING:
-        send(total_mine.at[0], total.at[0, here], all_send, all_recv.at[0], ring_row(d), col)
-    await_bytes(shares_b, sum_recv.at[1])
-    mine = partial[1:3, here]
-    for n in range(ring):
-        mine = mine + shares_b[n]
-    total_mine[1:3] = mine
-    total[1:3, here] = mine
-    for d in RING:
-        send(total_mine.at[1:3], total.at[1:3, here], all_send, all_recv.at[1], ring_row(d), col)
+    @pl.when(adds)
+    def _():
+        for block, slots in ((slice(0, 1), shares_tt), (slice(1, 3), shares_b)):
+            n_sem = block.start
+            await_bytes(slots.at[1, :ring], sum_recv.at[n_sem, 1])
+            mine = partial[block, here]
+            for n in range(ring):
+                mine = mine + slots[1, n].reshape(mine.shape)
+            total_mine[1, block] = mine
+            total[block, here] = mine
+            gather(1, total_mine.at[1, block], total.at[block, here], all_send, all_recv.at[n_sem])
+            await_bytes(slots.at[0], sum_recv.at[n_sem, 0])
+            mine = slots[0, 0].reshape(mine.shape)
+            for n in range(1, ring + 1):
+                mine = mine + slots[0, n].reshape(mine.shape)
+            total_mine[0, block] = mine
+            gather(0, total_mine.at[0, block], total.at[block, here], all_send, all_recv.at[n_sem])
+
     await_bytes(next_tops, next_recv.at[0])
     await_bytes(next_bottoms, next_recv.at[1])
     columns = parts_of(jnp.concatenate([top_now, bottom_now], axis=1))
     next_columns = parts_of(jnp.concatenate([next_tops[...], next_bottoms[...]], axis=1))
     between = product_of(columns, next_columns, FIRST)
-    await_bytes(total.at[0, : ring * share], all_recv.at[0])
-    await_bytes(total.at[1:3, : ring * share], all_recv.at[1])
+    def adding():
+        await_bytes(total.at[0:1, : ring * share], all_recv.at[0])
+        await_bytes(total.at[1:3, : ring * share], all_recv.at[1])
+
+    def plain():
+        await_bytes(total.at[0:1], all_recv.at[0])
+        await_bytes(total.at[1:3], all_recv.at[1])
+
+    by_core(adding, plain)
 
     cross = total[1]
     gram = jnp.concatenate(
@@ -292,23 +325,30 @@
         turns.append((turns_in[r, 0:1, :], turns_in[r, 1:2, :]))
         between = between * turns[r][0] + moved * turns[r][1]
     partial_tb[...] = full_product(rotation[:, :BLOCK], between[:, BLOCK:], FIRST)
-    for n, d in enumerate(RING):
-        send(partial_tb.at[ring_place(d)], shares_tb.at[n], sum2_send, sum2_recv, ring_row(d), col)
+    scatter(lambda place: partial_tb.at[place], shares_tb, sum2_send, sum2_recv)
     next_rotation = None
     for r in range(rounds):
         next_rotation = turned_by(next_rotation, first_plan(r), *turns[r])
     bottoms_in[...] = product_of(next_columns, [part[:, BLOCK:] for part in parts_of(next_rotation)])
     tops_now[...] = product_of(columns, [part[:, :BLOCK] for part in parts_of(rotation)])
-    await_bytes(shares_tb, sum2_recv)
-    mine = partial_tb[here]
-    for n in range(ring):
-        mine = mine + shares_tb[n]
-    total_tb_mine[...] = mine
-    total_tb[here] = mine
-    for d in RING:
-        send(total_tb_mine, total_tb.at[here], all2_send, all2_recv, ring_row(d), col)
+    @pl.when(adds)
+    def _():
+        await_bytes(shares_tb.at[1, :ring], sum2_recv.at[1])
+        mine = partial_tb[here]
+        for n in range(ring):
+            mine = mine + shares_tb[1, n]
+        total_tb_mine[1] = mine
+        total_tb[here] = mine
+        gather(1, total_tb_mine.at[1], total_tb.at[here], all2_send, all2_recv)
+        await_bytes(shares_tb.at[0], sum2_recv.at[0])
+        mine = shares_tb[0, 0]
+        for n in range(1, ring + 1):
+            mine = mine + shares_tb[0, n]
+        total_tb_mine[0] = mine
+        gather(0, total_tb_mine.at[0], total_tb.at[here], all2_send, all2_recv)
+
     await_bytes(square_in, next_recv.at[2 + rounds])
-    await_bytes(total_tb.at[: ring * share], all2_recv)
+    by_core(lambda: await_bytes(total_tb.at[: ring * share], all2_recv), lambda: await_bytes(total_tb, all2_recv))
     cross = total_tb[...]
     gram = jnp.concatenate(
         [jnp.concatenate([top_square, cross], axis=1), jnp.concatenate([jnp.transpose(cross), square_in[...]], axis=1)],
@@ -329,14 +369,23 @@
             result[2 * me] = now[:, :BLOCK]
     await_bytes(result.at[: 2 * near + 1], out_recv)
     await_bytes(x_own.at[: 2 * near], in_send)
-    await_bytes(tops.at[: 3 * ring * share], sum_send)
-    await_bytes(tops.at[: 3 * ring * share], all_send)
+
+    def adding():
+        await_bytes(tops.at[: 3 * ring * share], sum_send)
+        for _ in range(3):
+            await_bytes(tops.at[: (2 * ring + 1) * share], all_send)
+        await_bytes(tops.at[: ring * share], sum2_send)
+        await_bytes(tops.at[: (2 * ring + 1) * share], all2_send)
+
+    def plain():
+        await_bytes(tops.at[: 3 * ZS * share], sum_send)
+        await_bytes(tops.at[: ZS * share], sum2_send)
+
+    by_core(adding, plain)
     await_bytes(tops, next_send)
     await_bytes(bottoms, next_send)
     await_bytes(turns_out, next_send)
     await_bytes(square_out, next_send)
-    await_bytes(shares_tb, sum2_send)
-    await_bytes(shares_tb, all2_send)
     await_bytes(result.at[: 2 * near + 1], out_send)
 
 
@@ -360,10 +409,10 @@
             vmem((every, width), f32),
             vmem((every, width), f32),
             vmem((3, BLOCK, BLOCK), f32),
-            vmem((ring, share, BLOCK), f32),
-            vmem((ring, 2, share, BLOCK), f32),
+            vmem((2, ZS, 1, share, BLOCK), f32),
+            vmem((2, ZS, 2, share, BLOCK), f32),
             vmem((3, BLOCK, BLOCK), f32),
-            vmem((3, share, BLOCK), f32),
+            vmem((2, 3, share, BLOCK), f32),
             vmem((every, width), f32),
             vmem((every, width), f32),
             vmem((plan.shape[1], 2, WIDTH), f32),
@@ -373,21 +422,21 @@
             vmem((BLOCK, BLOCK), f32),
             vmem((every, width), f32),
             vmem((BLOCK, BLOCK), f32),
-            vmem((ring, share, BLOCK), f32),
+            vmem((2, ZS, share, BLOCK), f32),
             vmem((BLOCK, BLOCK), f32),
-            vmem((share, BLOCK), f32),
+            vmem((2, share, BLOCK), f32),
             vmem((near + 1, 2, chunk, width), f32),
             dma((3,)),
             dma,
             dma((2,)),
             dma,
+            dma((2, 2)),
+            dma,
             dma((2,)),
             dma,
+            dma((7,)),
+            dma,
             dma((2,)),
-            dma,
-            dma((7,)),
-            dma,
-            dma,
             dma,
             dma,
             dma,

time: 52.6 us -> 52.6 us (level)
  no operation moved by 1% of the time
where the time goes in v5:
time: 52.6 us; the launch traced here: 52.5 us
  Pallas kernels  51.3 us (98%)
  local copies, waits for them, and re-layouts  1.2 us (2%)
    pallas_call x1, Pallas kernels, body(): pl.pallas_call(kernel, out_shape=jax.ShapeDtypeStruct((slots, chunk, widt...  51.3 us
    reshape x1, local copies, waits for them, and re-layouts, body(): return result.transpose(1, 0, 2).reshape(matrix.shape)  1.2 us

profile of v5, /device:TPU:1, one launch (start us, length us, event | category | flops | bytes accessed | tf_op | source)
XLA Modules:
  0.0 52.5 jit_solution(9342551069244961731)
XLA Ops:
  0.0 51.3 %jacobi_steps.1 = f32[16,64,128]{2,1,0:T(8,128)S(1)} custom-call(f32[64,16,128]{2,1,0:T(8,128)} %bitcast.5, s32[2,4,256]{2,1,0:T(4,128)} %plan_hbm.1), custom_call_target="tpu_custom_call" | custom-call | flops 1000000000 | bytes 1048576 | tf_op jit(solution)/shard_map/jacobi_steps/pallas_call | solution.py:401
  51.3 1.2 %copy.3 = f32[64,8,2,128]{3,2,1,0:T(2,128)} copy(f32[64,8,2,128]{3,0,2,1:T(8,128)S(1)} %bitcast.4) | data formatting | bytes 1048576 | tf_op jit(solution)/shard_map/reshape | solution.py:449
